TPU v7x, 32 devices: a whole 2x2x4 slice. The times are simulated.
32 devices in a mesh: band: 8 (over y, x, core), pw: 4 (over z).
Axes of the slice: x: 2, y: 2, z: 4, core: 2. Of those that a mesh axis runs over, the one named last changes fastest.
Arguments:
- pair_density: bfloat16 [40, 128, 9216], P('band', None, 'pw'), may hold values from -6 to 6
- eigvecs: bfloat16 [2944, 9216], P('band', 'pw'), may hold values from -0.0625 to 0.0625
- screening: bfloat16 [2944, 2944], P('pw'), may hold values from -0.00048828125 to 0.00048828125
- occupation: float32 [16], replicated, may hold values from 0 to 1
- window_start: int32 [40], P('band'), may hold values from 0 to 511, as said below
- window_len: int32 [40], P('band'), may hold values from 1 to 128, as said below
- slot_band: int32 [40], P('band'), may hold values from -1 to 15, as said below
Outputs:
- sigma: float32 [512, 512], P(('band', 'pw'))
Inputs may be any that keep to these rules, and one draw needn't show every extreme that they name: window_start + window_len <= 512 for every slot. `window_len`: some slot has a window of 128 bands. On each index of band the live slots (slot_band >= 0) come first among its 5 slots; each index holds 3 to 5 live slots, and the counts of index i and index i + 8 / 2 add up to 8.
All inputs are finite; a program needn't handle non-finite values.
Results may differ from a plain program's by a relative error of at most 0.0049.
Values may be sent and summed in bfloat16 or wider, within the bound.
A program may use at most 128 MiB of HBM per device.

v0:
```python
import jax
import jax.numpy as jnp
from jax import lax
from jax.sharding import PartitionSpec as P

NB_SIGMA = 512


def per_device(pair_density, eigvecs, screening, occupation, window_start, window_len, slot_band):
    capacity, block, plane_rows = pair_density.shape
    density, starts, lengths, band_ids = (pair_density, window_start, window_len, slot_band)
    slots = density.shape[0]
    flat = density.reshape(slots * block, plane_rows)
    partial_proj = lax.dot_general(
        flat,
        lax.all_gather(eigvecs, "band", axis=0, tiled=True),
        (((1,), (1,)), ((), ())),
        preferred_element_type=jnp.float32,
    )
    row_ids = jnp.arange(block, dtype=jnp.int32)
    keep_rows = ((row_ids[None, :] < lengths[:, None]) & (band_ids[:, None] >= 0)).astype(
        jnp.float32
    )
    masked = partial_proj * keep_rows.reshape(slots * block, 1)
    projected = lax.psum(masked, "pw").astype(jnp.bfloat16)
    width = screening.shape[0]
    own_cols = lax.dynamic_slice_in_dim(projected, lax.axis_index("pw") * width, width, 1)
    screened = lax.dot_general(
        projected, screening, (((1,), (1,)), ((), ())), preferred_element_type=jnp.float32
    ).astype(jnp.bfloat16)
    block_sigma = lax.dot_general(
        screened.reshape(slots, block, width),
        own_cols.reshape(slots, block, width),
        (((2,), (2,)), ((0,), (0,))),
        preferred_element_type=jnp.float32,
    )
    band_list = jnp.arange(occupation.shape[0], dtype=jnp.int32)
    weights = 0.5 - jnp.sum(
        jnp.where(band_list[None, :] == band_ids[:, None], occupation[None, :], 0.0), axis=1
    )
    totals = jnp.zeros((NB_SIGMA + block, NB_SIGMA + block), jnp.float32)
    for index in range(slots):
        first = starts[index]
        previous = lax.dynamic_slice(totals, (first, first), (block, block))
        totals = lax.dynamic_update_slice(
            totals, previous + weights[index] * block_sigma[index], (first, first)
        )
    sigma_part = totals[:NB_SIGMA, :NB_SIGMA]
    by_band = lax.psum_scatter(sigma_part, "band", scatter_dimension=0, tiled=True)
    return lax.psum_scatter(by_band, "pw", scatter_dimension=0, tiled=True)


def solution(mesh):
    return jax.shard_map(
        per_device,
        mesh=mesh,
        in_specs=(
            P("band", None, "pw"),
            P("band", "pw"),
            P("pw", None),
            P(),
            P("band"),
            P("band"),
            P("band"),
        ),
        out_specs=P(("band", "pw"), None),
        check_vma=False,
    )
```

profile of v0, /device:TPU:0, one launch (start us, length us, event | category | flops | bytes accessed | tf_op | source)
XLA Modules:
  0.0 465.4 jit_solution(47097493405840025)
XLA Ops:
  6.5 0.7 all-gather.2.cloned.1.call-update
  7.3 0.0 reduce-scatter.3.cloned.1.call-start
  7.3 1.4 fusion.11
  17.9 0.9 select_reduce_fusion
  18.7 0.7 fusion.10
  19.4 0.7 broadcast_compare_fusion
  20.1 0.7 convert_bitcast_fusion
  20.8 67.3 %all-gather.2.cloned.1.call-done = bf16[2944,2304]{1,0:T(8,128)(2,1)} async-done(((bf16[368,2304]{1,0:T(8,128)(2,1)}), bf16[2944,2304]{1,0:T(8,128)(2,1)}) %all-gather.2.cloned.1.call-update) | async-done | bytes 13565968 | tf_op jit(solution)/shard_map/all_gather | solution.py:16
  88.1 0.0 copy-done
  88.1 14.4 %convolution_multiply_fusion = f32[640,2944]{1,0:T(8,128)} fusion(bf16[640,2304]{1,0:T(8,128)(2,1)S(1)} %bitcast.39, bf16[2944,2304]{1,0:T(8,128)(2,1)} %all-gather.2.cloned.1.call-done, f32[640]{0:T(1024)S(1)} %convert_bitcast_fusion), kind=kOutput, calls=%fused_computation | convolution fusion | flops 8684093440 | bytes 24054272 | tf_op jit(solution)/shard_map/dot_general | solution.py:14
  102.5 259.2 %all-reduce.1 = bf16[640,2944]{1,0:T(8,128)(2,1)} all-reduce(f32[640,2944]{1,0:T(8,128)} %convolution_multiply_fusion), channel_id=1, replica_groups=mesh['band'=8,'pw'=4] {'pw'}, use_global_device_ids=true, to_apply=%region_1.2 | all-reduce | flops 1884160 | bytes 11304960 | tf_op jit(solution)/shard_map/psum | solution.py:25
  361.7 2.7 constant_dynamic-slice_fusion
  364.4 8.0 %convolution_convert_fusion = bf16[640,736]{0,1:T(8,128)(2,1)} fusion(bf16[640,2944]{1,0:T(8,128)(2,1)} %all-reduce.1, bf16[736,2944]{1,0:T(8,128)(2,1)} %param.9), kind=kOutput, calls=%fused_computation.1 | convolution fusion | flops 2773954560 | bytes 9043968 | tf_op jit(solution)/shard_map/dot_general | solution.py:28
  372.4 2.2 copy.12
  374.7 1.9 fusion.12
  376.6 0.7 fusion.8
  377.3 1.3 broadcast_in_dim.10
  378.6 3.0 dynamic_update_slice.15
  381.6 1.6 fusion.7
  383.2 3.0 dynamic_update_slice.16
  386.2 1.7 fusion.5
  387.9 3.2 dynamic_update_slice.17
  391.1 1.6 fusion.3
  392.8 3.2 dynamic_update_slice.18
  395.9 1.6 fusion.1
  397.6 3.3 dynamic_update_slice.19
  400.8 2.2 slice.69
  403.1 0.0 reduce-scatter.3.cloned.1.call-update
  403.1 0.0 reduce-scatter.5.cloned.1.call-start
  403.2 33.9 %reduce-scatter.3.cloned.1.call-done = f32[64,512]{1,0:T(8,128)} async-done(((f32[512,512]{1,0:T(8,128)}), f32[64,512]{1,0:T(8,128)}) %reduce-scatter.3.cloned.1.call-update) | async-done | bytes 131088 | tf_op jit(solution)/shard_map/reduce_scatter | solution.py:49
  437.1 0.0 reduce-scatter.5.cloned.1.call-update
  437.1 21.7 %reduce-scatter.5.cloned.1.call-done = f32[16,512]{1,0:T(8,128)} async-done(((f32[64,512]{1,0:T(8,128)}), f32[16,512]{1,0:T(8,128)}) %reduce-scatter.5.cloned.1.call-update) | async-done | bytes 32784 | tf_op jit(solution)/shard_map/reduce_scatter | solution.py:50
  (3 shorter events, 0.0 us)
Async XLA Ops:
  6.5 81.6 %copy-start = (bf16[5,128,2304]{2,1,0:T(8,128)(2,1)S(1)}, bf16[5,128,2304]{2,1,0:T(8,128)(2,1)}, u32[]{:S(2)}) copy-start(bf16[5,128,2304]{2,1,0:T(8,128)(2,1)} %param.7) | copy-start | bytes 8847364
  6.5 81.6 %all-gather.2.cloned.1.call-start = ((), (), s32[]{:S(2)}) async-start(), calls=%async_computation.2 | async-start | bytes 15261696 | tf_op jit(solution)/shard_map/all_gather | solution.py:16
  7.3 429.8 %reduce-scatter.3.cloned.1.call-start = ((), (), s32[]{:S(2)}) async-start(), calls=%async_computation.3 | async-start | bytes 1179648 | tf_op jit(solution)/shard_map/reduce_scatter | solution.py:49
  403.1 55.8 %reduce-scatter.5.cloned.1.call-start = ((), (), s32[]{:S(2)}) async-start(), calls=%async_computation.4 | async-start | bytes 163840 | tf_op jit(solution)/shard_map/reduce_scatter | solution.py:50
Sparse Core Ops, SparseCore 0:
  9.2 78.8 all-gather.1
  403.2 33.8 reduce-scatter.2
  439.4 19.4 reduce-scatter.4
where the time goes:
time: 467 us; the launch traced here: 465 us
  blocking collectives  259 us (55%)
  waiting for transfers between devices  124 us (27%)
  local copies, waits for them, and re-layouts  26.3 us (6%)
  matrix products  24.3 us (5%)
  between operations  22.3 us (5%)
  other arithmetic  9.5 us (2%)
    psum x1, blocking collectives, per_device(): projected = lax.psum(masked, 'pw').astype(jnp.bfloat16)  259 us
    all_gather x1, waiting for transfers between devices, per_device(): lax.all_gather(eigvecs, 'band', axis=0, tiled=True)  67.3 us
    reduce_scatter x1, waiting for transfers between devices, per_device(): lax.psum_scatter(sigma_part, 'band', scatter_dimension=0, tiled=True)  33.9 us
    reduce_scatter x1, waiting for transfers between devices, per_device(): return lax.psum_scatter(by_band, 'pw', scatter_dimension=0, tiled=True)  21.7 us
    dynamic_update_slice x5, local copies, waits for them, and re-layouts, per_device(): lax.dynamic_update_slice(totals, previous + weights[index] * block_sigma[...  15.7 us
    dot_general x1, matrix products, per_device(): lax.dot_general(flat, lax.all_gather(eigvecs, 'band', axis=0, tiled=True)...  14.4 us
  transfers between devices with their start and end apart: 3, of which 3 were waited for; matrix products, arithmetic and copies ran while one was open for 1% of the time, Pallas kernels for 0%

commit v1 on v0

--- a/solution.py
+++ b/solution.py
@@ -1,12 +1,16 @@
+import functools
+
 import jax
 import jax.numpy as jnp
 from jax import lax
+from jax.experimental import pallas as pl
+from jax.experimental.pallas import tpu as pltpu
 from jax.sharding import PartitionSpec as P
 
 NB_SIGMA = 512
 
 
-def per_device(pair_density, eigvecs, screening, occupation, window_start, window_len, slot_band):
+def ring_per_device(pair_density, eigvecs, screening, occupation, window_start, window_len, slot_band):
     capacity, block, plane_rows = pair_density.shape
     density, starts, lengths, band_ids = (pair_density, window_start, window_len, slot_band)
     slots = density.shape[0]
@@ -50,9 +54,273 @@
     return lax.psum_scatter(by_band, "pw", scatter_dimension=0, tiled=True)
 
 
+def flip(index, relation):
+    total = 0
+    for place in (4, 2, 1):
+        bit = lax.rem(index // place, 2)
+        other = lax.rem(relation // place, 2)
+        total = total + place * (bit + other - 2 * bit * other)
+    return total
+
+
+def fused_kernel(
+    density_ref, eig_ref, screen_ref, keep_ref, weight_ref, out_ref,
+    eig, screen, part, sent, own, landed, proj, acc,
+    load_sem, eig_send, eig_recv, red_send, red_recv, up_send, up_recv, down_send, down_recv,
+):
+    mesh_id = pl.DeviceIdType.MESH
+    band, z = lax.axis_index("band"), lax.axis_index("pw")
+    n_rel, depth, _ = eig.shape
+    n_z = landed.shape[1] + 1
+    rows = own.shape[1]
+    slots, block, _ = out_ref.shape
+
+    barrier = pltpu.get_barrier_semaphore()
+    for rel in (1, 2, 4, 6):
+        pl.semaphore_signal(barrier, inc=1, device_id=(flip(band, rel), z), device_id_type=mesh_id)
+    for k in range(1, n_z):
+        pl.semaphore_signal(
+            barrier, inc=1, device_id=(band, lax.rem(z + k, n_z)), device_id_type=mesh_id
+        )
+    load = pltpu.make_async_copy(eig_ref, eig.at[0], load_sem)
+    load.start()
+    pl.semaphore_wait(barrier, 4 + n_z - 1)
+
+    def eig_copy(rel):
+        return pltpu.make_async_remote_copy(
+            src_ref=eig_ref, dst_ref=eig.at[rel], send_sem=eig_send.at[rel],
+            recv_sem=eig_recv.at[rel], device_id=(flip(band, rel), z), device_id_type=mesh_id,
+        )
+
+    def forward_copy(rel):
+        return pltpu.make_async_remote_copy(
+            src_ref=eig.at[rel], dst_ref=eig.at[rel + 1], send_sem=eig_send.at[rel + 1],
+            recv_sem=eig_recv.at[rel + 1], device_id=(flip(band, 1), z), device_id_type=mesh_id,
+        )
+
+    for rel in (1, 2, 4, 6):
+        eig_copy(rel).start()
+    for index in range(n_rel):
+        screen[index] = screen_ref[:, index * depth : (index + 1) * depth]
+    acc[...] = jnp.zeros_like(acc)
+    load.wait()
+
+    def red_copy(rel, k):
+        target = lax.rem(z + k, n_z)
+        return pltpu.make_async_remote_copy(
+            src_ref=sent.at[rel, target], dst_ref=landed.at[rel, k - 1],
+            send_sem=red_send.at[rel, k - 1], recv_sem=red_recv.at[rel, k - 1],
+            device_id=(band, target), device_id_type=mesh_id,
+        )
+
+    def up_copy(rel, hop):
+        source = lax.rem(z - hop + n_z, n_z)
+        return pltpu.make_async_remote_copy(
+            src_ref=proj.at[rel, source], dst_ref=proj.at[rel, source],
+            send_sem=up_send.at[rel, hop], recv_sem=up_recv.at[rel, hop],
+            device_id=(band, lax.rem(z + 1, n_z)), device_id_type=mesh_id,
+        )
+
+    def down_copy(rel, hop):
+        source = lax.rem(z + hop, n_z)
+        return pltpu.make_async_remote_copy(
+            src_ref=proj.at[rel, source], dst_ref=proj.at[rel, source],
+            send_sem=down_send.at[rel, hop], recv_sem=down_recv.at[rel, hop],
+            device_id=(band, lax.rem(z + n_z - 1, n_z)), device_id_type=mesh_id,
+        )
+
+    def landing(rel, hop, up):
+        source = lax.rem(z - hop - 1 + 2 * n_z, n_z) if up else lax.rem(z + hop + 1, n_z)
+        return pltpu.make_async_remote_copy(
+            src_ref=proj.at[rel, source], dst_ref=proj.at[rel, source],
+            send_sem=(up_send if up else down_send).at[rel, hop],
+            recv_sem=(up_recv if up else down_recv).at[rel, hop],
+            device_id=(band, lax.rem(z + 1, n_z)), device_id_type=mesh_id,
+        )
+
+    def pass_on(rel, hop):
+        @pl.when((z - hop >= 0) & (z + 1 < n_z))
+        def _():
+            up_copy(rel, hop).start()
+
+        @pl.when((z + hop < n_z) & (z >= 1))
+        def _():
+            down_copy(rel, hop).start()
+
+    def take(rel, hop):
+        @pl.when(z - hop - 1 >= 0)
+        def _():
+            landing(rel, hop, True).wait_recv()
+
+        @pl.when(z + hop + 1 < n_z)
+        def _():
+            landing(rel, hop, False).wait_recv()
+
+    def project(rel):
+        @pl.when(rel >= 1)
+        def _():
+            eig_copy(rel).wait_recv()
+
+        @pl.when((rel >= 2) & (lax.rem(rel, 2) == 0))
+        def _():
+            forward_copy(rel).start()
+
+        part[...] = lax.dot_general(
+            density_ref[...], eig[rel], (((1,), (1,)), ((), ())),
+            preferred_element_type=jnp.float32,
+        ).reshape(part.shape)
+        sent[rel] = part[...].astype(jnp.bfloat16)
+        own[rel] = part[z]
+        for k in (2, 1, 3):
+            red_copy(rel, k).start()
+
+    def reduce(rel):
+        for k in range(1, n_z):
+            red_copy(rel, k).wait_recv()
+        total = own[rel]
+        for k in range(1, n_z):
+            total = total + landed[rel, k - 1].astype(jnp.float32)
+        proj[rel, z] = (total * keep_ref[z]).astype(jnp.bfloat16)
+        pass_on(rel, 0)
+
+    def screen_step(rel):
+        take(rel, n_z - 2)
+        whole = proj[rel].reshape(n_z * rows, depth)
+        at = flip(band, rel)
+        for half in range(2):
+            acc[half] += lax.dot_general(
+                whole, screen[at, half * depth : (half + 1) * depth], (((1,), (1,)), ((), ())),
+                preferred_element_type=jnp.float32,
+            )
+
+    def step(t, carry):
+        @pl.when(t < n_rel)
+        def _():
+            project(t)
+
+        @pl.when((t >= 1) & (t < n_rel + 1))
+        def _():
+            reduce(t - 1)
+
+        for hop in range(n_z - 2):
+            @pl.when((t >= 2 + hop) & (t < n_rel + 2 + hop))
+            def _():
+                take(t - 2 - hop, hop)
+                pass_on(t - 2 - hop, hop + 1)
+
+        @pl.when(t >= n_z)
+        def _():
+            screen_step(t - n_z)
+
+        return carry
+
+    lax.fori_loop(0, n_rel + n_z, step, 0)
+
+    screened = acc[...].astype(jnp.bfloat16)
+    pairs = [proj[flip(band, 2 * z + half)].reshape(n_z * rows, depth) for half in range(2)]
+    for slot in range(slots):
+        here = slice(slot * block, (slot + 1) * block)
+        total = 0.0
+        for half in range(2):
+            total = total + lax.dot_general(
+                screened[half, here], pairs[half][here], (((1,), (1,)), ((), ())),
+                preferred_element_type=jnp.float32,
+            )
+        out_ref[slot] = total * weight_ref[slot]
+
+    for rel in (1, 2, 4, 6):
+        eig_copy(rel).wait_send()
+    for rel in (2, 4, 6):
+        forward_copy(rel).wait_send()
+
+    def drain(rel, carry):
+        for k in range(1, n_z):
+            red_copy(rel, k).wait_send()
+        for hop in range(n_z - 1):
+            @pl.when((z - hop >= 0) & (z + 1 < n_z))
+            def _():
+                up_copy(rel, hop).wait_send()
+
+            @pl.when((z + hop < n_z) & (z >= 1))
+            def _():
+                down_copy(rel, hop).wait_send()
+        return carry
+
+    lax.fori_loop(0, n_rel, drain, 0)
+
+
+def per_device(
+    n_z, n_rel, pair_density, eigvecs, screening, occupation, window_start, window_len, slot_band
+):
+    slots, block, plane_rows = pair_density.shape
+    depth, width = eigvecs.shape[0], screening.shape[0]
+    rows = slots * block // n_z
+    keep_rows = (
+        (jnp.arange(block, dtype=jnp.int32)[None, :] < window_len[:, None])
+        & (slot_band[:, None] >= 0)
+    ).astype(jnp.float32)
+    band_list = jnp.arange(occupation.shape[0], dtype=jnp.int32)
+    weights = 0.5 - jnp.sum(
+        jnp.where(band_list[None, :] == slot_band[:, None], occupation[None, :], 0.0), axis=1
+    )
+    dma = pltpu.SemaphoreType.DMA
+    vmem = pl.BlockSpec(memory_space=pltpu.VMEM)
+    block_sigma = pl.pallas_call(
+        fused_kernel,
+        out_shape=jax.ShapeDtypeStruct((slots, block, block), jnp.float32),
+        in_specs=[vmem, pl.BlockSpec(memory_space=pl.ANY), vmem, vmem, vmem],
+        out_specs=vmem,
+        scratch_shapes=[
+            pltpu.VMEM((n_rel, depth, plane_rows), jnp.bfloat16),
+            pltpu.VMEM((n_rel, width, depth), jnp.bfloat16),
+            pltpu.VMEM((n_z, rows, depth), jnp.float32),
+            pltpu.VMEM((n_rel, n_z, rows, depth), jnp.bfloat16),
+            pltpu.VMEM((n_rel, rows, depth), jnp.float32),
+            pltpu.VMEM((n_rel, n_z - 1, rows, depth), jnp.bfloat16),
+            pltpu.VMEM((n_rel, n_z, rows, depth), jnp.bfloat16),
+            pltpu.VMEM((2, slots * block, depth), jnp.float32),
+            dma,
+            dma((n_rel,)),
+            dma((n_rel,)),
+            dma((n_rel, n_z - 1)),
+            dma((n_rel, n_z - 1)),
+            dma((n_rel, n_z - 1)),
+            dma((n_rel, n_z - 1)),
+            dma((n_rel, n_z - 1)),
+            dma((n_rel, n_z - 1)),
+        ],
+        compiler_params=pltpu.CompilerParams(
+            collective_id=0, has_side_effects=True, vmem_limit_bytes=60 * 2**20
+        ),
+    )(
+        pair_density.reshape(slots * block, plane_rows),
+        eigvecs,
+        screening,
+        keep_rows.reshape(n_z, rows, 1),
+        jnp.broadcast_to(weights[:, None, None], (slots, 8, block))[:, :1],
+    )
+    return finish(block_sigma, window_start)
+
+
+def finish(block_sigma, window_start):
+    slots, block, _ = block_sigma.shape
+    totals = jnp.zeros((NB_SIGMA + block, NB_SIGMA + block), jnp.float32)
+    for index in range(slots):
+        first = window_start[index]
+        previous = lax.dynamic_slice(totals, (first, first), (block, block))
+        totals = lax.dynamic_update_slice(totals, previous + block_sigma[index], (first, first))
+    sigma_part = totals[:NB_SIGMA, :NB_SIGMA]
+    by_band = lax.psum_scatter(sigma_part, "band", scatter_dimension=0, tiled=True)
+    return lax.psum_scatter(by_band, "pw", scatter_dimension=0, tiled=True)
+
+
 def solution(mesh):
+    n_band, n_z = mesh.shape["band"], mesh.shape["pw"]
+    body = ring_per_device
+    if n_band == 8 and n_z == 4:
+        body = functools.partial(per_device, n_z, n_band)
     return jax.shard_map(
-        per_device,
+        body,
         mesh=mesh,
         in_specs=(
             P("band", None, "pw"),

time: 467 us -> 258 us (0.55)
  blocking collectives: 259 us -> 0 us
  Pallas kernels: 0 us -> 161 us
  waiting for transfers between devices: 124 us -> 56.2 us
  matrix products: 24.3 us -> 0 us
  local copies, waits for them, and re-layouts: 26.3 us -> 14.8 us
  other arithmetic: 9.5 us -> 2.64 us
    psum x1 -> x0, blocking collectives: 259 us -> none  [per_device(): projected = lax.psum(masked, 'pw').astype(jnp.bfloat16)]
    pallas_call x0 -> x1, Pallas kernels: none -> 161 us  [per_device(): pl.pallas_call(fused_kernel, out_shape=jax.ShapeDtypeStruct((slots, block...]
    all_gather x1 -> x0, waiting for transfers between devices: 67.3 us -> none  [per_device(): lax.all_gather(eigvecs, 'band', axis=0, tiled=True)]
    dot_general x3 -> x0, matrix products: 24.3 us -> none  [the longest x1 14.4 us: per_device(): lax.dot_general(flat, lax.all_gather(eigvecs, 'band', axis=0, tiled=True)...]
    add x4, other arithmetic: 6.53 us -> 0.39 us  [finish(): previous + block_sigma[index]]
    dynamic_update_slice x5, local copies, waits for them, and re-layouts: 15.7 us -> 9.59 us  [finish(): lax.dynamic_update_slice(totals, previous + block_sigma[index], (first, f...]
  transfers between devices with their start and end apart: 3 -> 2, of which waited for: 3 -> 2; matrix products, arithmetic and copies ran while one was open for 1% -> 0% of each run, Pallas kernels for 0% -> 0%
where the time goes in v1:
time: 258 us
  Pallas kernels  161 us (62%)
  waiting for transfers between devices  56.2 us (22%)
  between operations  22.8 us (9%)
  local copies, waits for them, and re-layouts  14.8 us (6%)
  other arithmetic  2.64 us (1%)
    pallas_call x1, Pallas kernels, per_device(): pl.pallas_call(fused_kernel, out_shape=jax.ShapeDtypeStruct((slots, block...  161 us
    reduce_scatter x1, waiting for transfers between devices, finish(): lax.psum_scatter(sigma_part, 'band', scatter_dimension=0, tiled=True)  34.5 us
    reduce_scatter x1, waiting for transfers between devices, finish(): return lax.psum_scatter(by_band, 'pw', scatter_dimension=0, tiled=True)  21.7 us
    dynamic_update_slice x5, local copies, waits for them, and re-layouts, finish(): lax.dynamic_update_slice(totals, previous + block_sigma[index], (first, f...  9.59 us
  transfers between devices with their start and end apart: 2, of which 2 were waited for; matrix products, arithmetic and copies ran while one was open for 0% of the time, Pallas kernels for 0%

profile of v1, /device:TPU:0, one launch (start us, length us, event | category | flops | bytes accessed | tf_op | source)
XLA Modules:
  0.0 257.6 jit_solution(13475397850738205871)
XLA Ops:
  6.5 0.0 reduce-scatter.3.cloned.1.call-start
  6.5 1.5 fusion.2
  14.2 0.7 broadcast_compare_fusion
  14.8 0.9 select_reduce_fusion
  15.7 0.7 fusion.1
  16.4 1.0 reshape.54.keep_ref
  17.4 0.6 slice.36.weight_ref
  18.1 161.1 %shard_map.73 = f32[5,128,128]{2,1,0:T(8,128)} custom-call(bf16[640,2304]{1,0:T(8,128)(2,1)} %bitcast.16, bf16[368,2304]{1,0:T(8,128)(2,1)} %eig_ref.1, bf16[736,2944]{1,0:T(8,128)(2,1)} %screen_ref.1, f32[4,160,1]{2,1,0:T(8,128)} %reshape.54.keep_ref, f32[5,1,128]{2,1,0:T(1,128)} %slice.36.weight_ref), custom_call_target="tpu_custom_call" | custom-call | tf_op jit(solution)/shard_map/pallas_call | solution.py:268
  179.1 0.0 copy-start
  179.1 0.9 slice_bitcast_fusion
  181.3 0.1 broadcast_in_dim.10
  181.4 1.7 dynamic_update_slice.15
  183.1 0.0 copy-done
  183.1 0.1 bitcast_add_fusion.3
  183.2 1.7 dynamic_update_slice.16
  185.5 0.1 bitcast_add_fusion.2
  185.6 2.1 dynamic_update_slice.17
  188.3 0.1 bitcast_add_fusion.1
  188.4 2.1 dynamic_update_slice.18
  191.1 0.1 bitcast_add_fusion
  191.2 2.1 dynamic_update_slice.19
  193.3 1.1 slice.48
  194.4 0.0 reduce-scatter.3.cloned.1.call-update
  194.5 0.0 reduce-scatter.5.cloned.1.call-start
  194.5 34.5 %reduce-scatter.3.cloned.1.call-done = f32[64,512]{1,0:T(8,128)} async-done(((f32[512,512]{1,0:T(8,128)}), f32[64,512]{1,0:T(8,128)}) %reduce-scatter.3.cloned.1.call-update) | async-done | bytes 131088 | tf_op jit(solution)/shard_map/reduce_scatter | solution.py:313
  229.0 0.0 reduce-scatter.5.cloned.1.call-update
  229.0 21.7 %reduce-scatter.5.cloned.1.call-done = f32[16,512]{1,0:T(8,128)} async-done(((f32[64,512]{1,0:T(8,128)}), f32[16,512]{1,0:T(8,128)}) %reduce-scatter.5.cloned.1.call-update) | async-done | bytes 32784 | tf_op jit(solution)/shard_map/reduce_scatter | solution.py:314
  (1 shorter events, 0.0 us)
Async XLA Ops:
  6.5 222.5 %reduce-scatter.3.cloned.1.call-start = ((), (), s32[]{:S(2)}) async-start(), calls=%async_computation.2 | async-start | bytes 1179648 | tf_op jit(solution)/shard_map/reduce_scatter | solution.py:313
  179.1 3.9 %copy-start = (f32[5,128,128]{2,1,0:T(8,128)S(1)}, f32[5,128,128]{2,1,0:T(8,128)}, u32[]{:S(2)}) copy-start(f32[5,128,128]{2,1,0:T(8,128)} %shard_map.73) | copy-start | bytes 983044
  194.5 56.2 %reduce-scatter.5.cloned.1.call-start = ((), (), s32[]{:S(2)}) async-start(), calls=%async_computation.3 | async-start | bytes 163840 | tf_op jit(solution)/shard_map/reduce_scatter | solution.py:314
Sparse Core Ops, SparseCore 0:
  194.6 34.3 reduce-scatter.2
  231.2 19.4 reduce-scatter.4

commit v2 on v1

--- a/solution.py
+++ b/solution.py
@@ -63,20 +63,27 @@
     return total
 
 
+def split(value):
+    top = value.astype(jnp.bfloat16)
+    return top, (value - top.astype(jnp.float32)).astype(jnp.bfloat16)
+
+
 def fused_kernel(
-    density_ref, eig_ref, screen_ref, keep_ref, weight_ref, out_ref,
+    density_ref, eig_ref, screen_ref, keep_ref, weight_ref, start_ref, out_ref,
     eig, screen, part, sent, own, landed, proj, acc,
+    place, high, low, sigma, band_sum, sigma_in, band_in,
     load_sem, eig_send, eig_recv, red_send, red_recv, up_send, up_recv, down_send, down_recv,
+    sig_send, sig_recv, fin_send, fin_recv,
 ):
     mesh_id = pl.DeviceIdType.MESH
     band, z = lax.axis_index("band"), lax.axis_index("pw")
     n_rel, depth, _ = eig.shape
     n_z = landed.shape[1] + 1
     rows = own.shape[1]
-    slots, block, _ = out_ref.shape
+    slots, block = weight_ref.shape[0], weight_ref.shape[2]
 
     barrier = pltpu.get_barrier_semaphore()
-    for rel in (1, 2, 4, 6):
+    for rel in range(1, n_rel):
         pl.semaphore_signal(barrier, inc=1, device_id=(flip(band, rel), z), device_id_type=mesh_id)
     for k in range(1, n_z):
         pl.semaphore_signal(
@@ -84,7 +91,7 @@
         )
     load = pltpu.make_async_copy(eig_ref, eig.at[0], load_sem)
     load.start()
-    pl.semaphore_wait(barrier, 4 + n_z - 1)
+    pl.semaphore_wait(barrier, n_rel - 1 + n_z - 1)
 
     def eig_copy(rel):
         return pltpu.make_async_remote_copy(
@@ -226,7 +233,58 @@
                 screened[half, here], pairs[half][here], (((1,), (1,)), ((), ())),
                 preferred_element_type=jnp.float32,
             )
-        out_ref[slot] = total * weight_ref[slot]
+        total = total * weight_ref[slot]
+        bands = lax.broadcasted_iota(jnp.int32, (place.shape[0], block), 0)
+        window = start_ref[slot] + lax.broadcasted_iota(jnp.int32, (place.shape[0], block), 1)
+        onehot = jnp.where(bands == window, 1.0, 0.0).astype(jnp.bfloat16)
+        place[:, here] = onehot
+        spread = 0.0
+        for piece in split(total):
+            spread = spread + jnp.dot(onehot, piece, preferred_element_type=jnp.float32)
+        high[:, here], low[:, here] = split(spread)
+
+    whole = 0.0
+    for piece in (high, low):
+        whole = whole + lax.dot_general(
+            piece[...], place[...], (((1,), (1,)), ((), ())), preferred_element_type=jnp.float32
+        )
+    sigma[...] = whole.reshape(sigma.shape)
+
+    def sigma_copy(rel):
+        target = flip(band, rel)
+        return pltpu.make_async_remote_copy(
+            src_ref=sigma.at[target], dst_ref=sigma_in.at[rel - 1],
+            send_sem=sig_send.at[rel - 1], recv_sem=sig_recv.at[rel - 1],
+            device_id=(target, z), device_id_type=mesh_id,
+        )
+
+    def final_copy(k):
+        target = lax.rem(z + k, n_z)
+        return pltpu.make_async_remote_copy(
+            src_ref=band_sum.at[target], dst_ref=band_in.at[k - 1],
+            send_sem=fin_send.at[k - 1], recv_sem=fin_recv.at[k - 1],
+            device_id=(band, target), device_id_type=mesh_id,
+        )
+
+    for rel in (6, 7, 2, 4, 3, 5, 1):
+        sigma_copy(rel).start()
+    total = sigma[band]
+    for rel in range(1, n_rel):
+        sigma_copy(rel).wait_recv()
+        total = total + sigma_in[rel - 1]
+    band_sum[...] = total.reshape(band_sum.shape)
+    for k in (2, 1, 3):
+        final_copy(k).start()
+    total = band_sum[z]
+    for k in range(1, n_z):
+        final_copy(k).wait_recv()
+        total = total + band_in[k - 1]
+    out_ref[...] = total
+
+    for rel in range(1, n_rel):
+        sigma_copy(rel).wait_send()
+    for k in range(1, n_z):
+        final_copy(k).wait_send()
 
     for rel in (1, 2, 4, 6):
         eig_copy(rel).wait_send()
@@ -265,10 +323,14 @@
     )
     dma = pltpu.SemaphoreType.DMA
     vmem = pl.BlockSpec(memory_space=pltpu.VMEM)
-    block_sigma = pl.pallas_call(
+    strip = NB_SIGMA // (n_rel * n_z)
+    return pl.pallas_call(
         fused_kernel,
-        out_shape=jax.ShapeDtypeStruct((slots, block, block), jnp.float32),
-        in_specs=[vmem, pl.BlockSpec(memory_space=pl.ANY), vmem, vmem, vmem],
+        out_shape=jax.ShapeDtypeStruct((strip, NB_SIGMA), jnp.float32),
+        in_specs=[
+            vmem, pl.BlockSpec(memory_space=pl.ANY), vmem, vmem, vmem,
+            pl.BlockSpec(memory_space=pltpu.SMEM),
+        ],
         out_specs=vmem,
         scratch_shapes=[
             pltpu.VMEM((n_rel, depth, plane_rows), jnp.bfloat16),
@@ -279,6 +341,13 @@
             pltpu.VMEM((n_rel, n_z - 1, rows, depth), jnp.bfloat16),
             pltpu.VMEM((n_rel, n_z, rows, depth), jnp.bfloat16),
             pltpu.VMEM((2, slots * block, depth), jnp.float32),
+            pltpu.VMEM((NB_SIGMA, slots * block), jnp.bfloat16),
+            pltpu.VMEM((NB_SIGMA, slots * block), jnp.bfloat16),
+            pltpu.VMEM((NB_SIGMA, slots * block), jnp.bfloat16),
+            pltpu.VMEM((n_rel, n_z * strip, NB_SIGMA), jnp.float32),
+            pltpu.VMEM((n_z, strip, NB_SIGMA), jnp.float32),
+            pltpu.VMEM((n_rel - 1, n_z * strip, NB_SIGMA), jnp.float32),
+            pltpu.VMEM((n_z - 1, strip, NB_SIGMA), jnp.float32),
             dma,
             dma((n_rel,)),
             dma((n_rel,)),
@@ -288,6 +357,10 @@
             dma((n_rel, n_z - 1)),
             dma((n_rel, n_z - 1)),
             dma((n_rel, n_z - 1)),
+            dma((n_rel - 1,)),
+            dma((n_rel - 1,)),
+            dma((n_z - 1,)),
+            dma((n_z - 1,)),
         ],
         compiler_params=pltpu.CompilerParams(
             collective_id=0, has_side_effects=True, vmem_limit_bytes=60 * 2**20
@@ -298,20 +371,8 @@
         screening,
         keep_rows.reshape(n_z, rows, 1),
         jnp.broadcast_to(weights[:, None, None], (slots, 8, block))[:, :1],
-    )
-    return finish(block_sigma, window_start)
-
-
-def finish(block_sigma, window_start):
-    slots, block, _ = block_sigma.shape
-    totals = jnp.zeros((NB_SIGMA + block, NB_SIGMA + block), jnp.float32)
-    for index in range(slots):
-        first = window_start[index]
-        previous = lax.dynamic_slice(totals, (first, first), (block, block))
-        totals = lax.dynamic_update_slice(totals, previous + block_sigma[index], (first, first))
-    sigma_part = totals[:NB_SIGMA, :NB_SIGMA]
-    by_band = lax.psum_scatter(sigma_part, "band", scatter_dimension=0, tiled=True)
-    return lax.psum_scatter(by_band, "pw", scatter_dimension=0, tiled=True)
+        window_start,
+    )
 
 
 def solution(mesh):

time: 258 us -> 184 us (0.71)
  waiting for transfers between devices: 56.2 us -> 0 us
  between operations: 22.8 us -> 0.01 us
  Pallas kernels: 161 us -> 178 us
  local copies, waits for them, and re-layouts: 14.8 us -> 2.97 us
    reduce_scatter x2 -> x0, waiting for transfers between devices: 56.2 us -> none  [the longest x1 34.5 us: finish(): lax.psum_scatter(sigma_part, 'band', scatter_dimension=0, tiled=True)]
    pallas_call x1, Pallas kernels: 161 us -> 178 us  [per_device(): pl.pallas_call(fused_kernel, out_shape=jax.ShapeDtypeStruct((strip, NB_SI...]
    dynamic_update_slice x5 -> x0, local copies, waits for them, and re-layouts: 9.59 us -> none  [finish(): lax.dynamic_update_slice(totals, previous + block_sigma[index], (first, f...]
    slice x2 -> x0, local copies, waits for them, and re-layouts: 2.61 us -> none  [the longest x1 1.48 us: finish(): first = window_start[index]]
  transfers between devices with their start and end apart: 2 -> 0, of which waited for: 2 -> 0; matrix products, arithmetic and copies ran while one was open for 0% -> 0% of each run, Pallas kernels for 0% -> 0%
where the time goes in v2:
time: 184 us; the launch traced here: 183 us
  Pallas kernels  178 us (97%)
  local copies, waits for them, and re-layouts  2.97 us (2%)
  other arithmetic  2.25 us (1%)
    pallas_call x1, Pallas kernels, per_device(): pl.pallas_call(fused_kernel, out_shape=jax.ShapeDtypeStruct((strip, NB_SI...  178 us

profile of v2, /device:TPU:0, one launch (start us, length us, event | category | flops | bytes accessed | tf_op | source)
XLA Modules:
  0.0 183.2 jit_solution(16974088597218216908)
XLA Ops:
  0.0 0.9 select_reduce_fusion
  0.9 0.7 broadcast_compare_fusion
  1.5 0.6 slice.3.weight_ref
  2.2 0.7 fusion.1
  2.9 0.9 reshape.54.keep_ref
  3.9 178.0 %shard_map.73 = f32[16,512]{1,0:T(8,128)} custom-call(bf16[640,2304]{1,0:T(8,128)(2,1)} %bitcast.1, bf16[368,2304]{1,0:T(8,128)(2,1)} %eig_ref.1, bf16[736,2944]{1,0:T(8,128)(2,1)} %screen_ref.1, f32[4,160,1]{2,1,0:T(8,128)} %reshape.54.keep_ref, f32[5,1,128]{2,1,0:T(1,128)} %slice.3.weight_ref, s32[5]{0:T(128)} %start_ref.1), custom_call_target="tpu_custom_call" | custom-call | tf_op jit(solution)/shard_map/pallas_call | solution.py:327
  181.9 1.4 copy.11
  (1 shorter events, 0.0 us)

commit v3 on v2

--- a/solution.py
+++ b/solution.py
@@ -69,10 +69,10 @@
 
 
 def fused_kernel(
-    density_ref, eig_ref, screen_ref, keep_ref, weight_ref, start_ref, out_ref,
-    eig, screen, part, sent, own, landed, proj, acc,
+    density_ref, eig_ref, screen_ref, meta_ref, out_ref,
+    density, extra, extra_meta, meta, eig, screen, part, sent, own, landed, proj, acc,
     place, high, low, sigma, band_sum, sigma_in, band_in,
-    load_sem, eig_send, eig_recv, red_send, red_recv, up_send, up_recv, down_send, down_recv,
+    load_sem, extra_send, extra_recv, eig_send, eig_recv, red_send, red_recv, up_send, up_recv, down_send, down_recv,
     sig_send, sig_recv, fin_send, fin_recv,
 ):
     mesh_id = pl.DeviceIdType.MESH
@@ -80,7 +80,8 @@
     n_rel, depth, _ = eig.shape
     n_z = landed.shape[1] + 1
     rows = own.shape[1]
-    slots, block = weight_ref.shape[0], weight_ref.shape[2]
+    slots, block = n_z, rows
+    last = slots * block
 
     barrier = pltpu.get_barrier_semaphore()
     for rel in range(1, n_rel):
@@ -89,8 +90,12 @@
         pl.semaphore_signal(
             barrier, inc=1, device_id=(band, lax.rem(z + k, n_z)), device_id_type=mesh_id
         )
-    load = pltpu.make_async_copy(eig_ref, eig.at[0], load_sem)
-    load.start()
+    loads = [
+        pltpu.make_async_copy(density_ref.at[pl.ds(0, last)], density, load_sem.at[0]),
+        pltpu.make_async_copy(eig_ref, eig.at[0], load_sem.at[1]),
+    ]
+    for load in loads:
+        load.start()
     pl.semaphore_wait(barrier, n_rel - 1 + n_z - 1)
 
     def eig_copy(rel):
@@ -105,13 +110,20 @@
             recv_sem=eig_recv.at[rel + 1], device_id=(flip(band, 1), z), device_id_type=mesh_id,
         )
 
+    partner = (flip(band, n_rel // 2), z)
+    swaps = [
+        pltpu.make_async_remote_copy(
+            src_ref=source, dst_ref=target, send_sem=extra_send.at[index],
+            recv_sem=extra_recv.at[index], device_id=partner, device_id_type=mesh_id,
+        )
+        for index, (source, target) in enumerate(
+            [(density_ref.at[pl.ds(last, block)], extra), (meta_ref.at[slots], extra_meta)]
+        )
+    ]
+    for swap in swaps:
+        swap.start()
     for rel in (1, 2, 4, 6):
         eig_copy(rel).start()
-    for index in range(n_rel):
-        screen[index] = screen_ref[:, index * depth : (index + 1) * depth]
-    acc[...] = jnp.zeros_like(acc)
-    load.wait()
-
     def red_copy(rel, k):
         target = lax.rem(z + k, n_z)
         return pltpu.make_async_remote_copy(
@@ -163,6 +175,25 @@
         def _():
             landing(rel, hop, False).wait_recv()
 
+    def multiply(rel, first, stop):
+        result = lax.dot_general(
+            density[first * block : stop * block], eig[rel], (((1,), (1,)), ((), ())),
+            preferred_element_type=jnp.float32,
+        ).reshape(stop - first, block, depth)
+        part[first:stop] = result
+        sent[rel, first:stop] = result.astype(jnp.bfloat16)
+
+        @pl.when((z >= first) & (z < stop))
+        def _():
+            own[rel] = part[z]
+
+        for k in (2, 1, 3):
+            target = lax.rem(z + k, n_z)
+
+            @pl.when((target >= first) & (target < stop))
+            def _():
+                red_copy(rel, k).start()
+
     def project(rel):
         @pl.when(rel >= 1)
         def _():
@@ -172,14 +203,21 @@
         def _():
             forward_copy(rel).start()
 
-        part[...] = lax.dot_general(
-            density_ref[...], eig[rel], (((1,), (1,)), ((), ())),
-            preferred_element_type=jnp.float32,
-        ).reshape(part.shape)
-        sent[rel] = part[...].astype(jnp.bfloat16)
-        own[rel] = part[z]
-        for k in (2, 1, 3):
-            red_copy(rel, k).start()
+        @pl.when(rel == 0)
+        def _():
+            for swap in swaps:
+                swap.wait_recv()
+            taken = meta_ref[slots - 1, 0:1, 0:1] > 0.0
+            for slot in range(slots - 1):
+                meta[slot] = meta_ref[slot]
+            meta[slots - 1] = jnp.where(taken, meta_ref[slots - 1], extra_meta[...])
+            tail = density[last - block :]
+            density[last - block :] = jnp.where(taken, tail, extra[...])
+            multiply(rel, slots - 1, slots)
+
+        @pl.when(rel > 0)
+        def _():
+            multiply(rel, 0, slots)
 
     def reduce(rel):
         for k in range(1, n_z):
@@ -187,7 +225,9 @@
         total = own[rel]
         for k in range(1, n_z):
             total = total + landed[rel, k - 1].astype(jnp.float32)
-        proj[rel, z] = (total * keep_ref[z]).astype(jnp.bfloat16)
+        row_ids = lax.broadcasted_iota(jnp.int32, total.shape, 0).astype(jnp.float32)
+        keep = jnp.where(row_ids < meta[z, 0:1, 0:1], 1.0, 0.0)
+        proj[rel, z] = (total * keep).astype(jnp.bfloat16)
         pass_on(rel, 0)
 
     def screen_step(rel):
@@ -221,6 +261,12 @@
 
         return carry
 
+    for load in loads:
+        load.wait()
+    multiply(0, 0, slots - 1)
+    for index in range(n_rel):
+        screen[index] = screen_ref[:, index * depth : (index + 1) * depth]
+    acc[...] = jnp.zeros_like(acc)
     lax.fori_loop(0, n_rel + n_z, step, 0)
 
     screened = acc[...].astype(jnp.bfloat16)
@@ -233,9 +279,10 @@
                 screened[half, here], pairs[half][here], (((1,), (1,)), ((), ())),
                 preferred_element_type=jnp.float32,
             )
-        total = total * weight_ref[slot]
-        bands = lax.broadcasted_iota(jnp.int32, (place.shape[0], block), 0)
-        window = start_ref[slot] + lax.broadcasted_iota(jnp.int32, (place.shape[0], block), 1)
+        total = total * meta[slot, 1:2]
+        bands = lax.broadcasted_iota(jnp.int32, (place.shape[0], block), 0).astype(jnp.float32)
+        window = lax.broadcasted_iota(jnp.int32, (place.shape[0], block), 1).astype(jnp.float32)
+        window = window + meta[slot, 2:3]
         onehot = jnp.where(bands == window, 1.0, 0.0).astype(jnp.bfloat16)
         place[:, here] = onehot
         spread = 0.0
@@ -286,6 +333,8 @@
     for k in range(1, n_z):
         final_copy(k).wait_send()
 
+    for swap in swaps:
+        swap.wait_send()
     for rel in (1, 2, 4, 6):
         eig_copy(rel).wait_send()
     for rel in (2, 4, 6):
@@ -310,17 +359,16 @@
 def per_device(
     n_z, n_rel, pair_density, eigvecs, screening, occupation, window_start, window_len, slot_band
 ):
-    slots, block, plane_rows = pair_density.shape
+    capacity, block, plane_rows = pair_density.shape
     depth, width = eigvecs.shape[0], screening.shape[0]
-    rows = slots * block // n_z
-    keep_rows = (
-        (jnp.arange(block, dtype=jnp.int32)[None, :] < window_len[:, None])
-        & (slot_band[:, None] >= 0)
-    ).astype(jnp.float32)
+    slots, rows = n_z, block
+    kept = jnp.where(slot_band >= 0, window_len, 0).astype(jnp.float32)
     band_list = jnp.arange(occupation.shape[0], dtype=jnp.int32)
     weights = 0.5 - jnp.sum(
         jnp.where(band_list[None, :] == slot_band[:, None], occupation[None, :], 0.0), axis=1
     )
+    fields = jnp.stack([kept, weights, window_start.astype(jnp.float32)], axis=1)
+    meta = jnp.broadcast_to(jnp.pad(fields, ((0, 0), (0, 5)))[:, :, None], (capacity, 8, block))
     dma = pltpu.SemaphoreType.DMA
     vmem = pl.BlockSpec(memory_space=pltpu.VMEM)
     strip = NB_SIGMA // (n_rel * n_z)
@@ -328,11 +376,14 @@
         fused_kernel,
         out_shape=jax.ShapeDtypeStruct((strip, NB_SIGMA), jnp.float32),
         in_specs=[
-            vmem, pl.BlockSpec(memory_space=pl.ANY), vmem, vmem, vmem,
-            pl.BlockSpec(memory_space=pltpu.SMEM),
+            pl.BlockSpec(memory_space=pl.ANY), pl.BlockSpec(memory_space=pl.ANY), vmem, vmem,
         ],
         out_specs=vmem,
         scratch_shapes=[
+            pltpu.VMEM((slots * block, plane_rows), jnp.bfloat16),
+            pltpu.VMEM((block, plane_rows), jnp.bfloat16),
+            pltpu.VMEM((8, block), jnp.float32),
+            pltpu.VMEM((slots, 8, block), jnp.float32),
             pltpu.VMEM((n_rel, depth, plane_rows), jnp.bfloat16),
             pltpu.VMEM((n_rel, width, depth), jnp.bfloat16),
             pltpu.VMEM((n_z, rows, depth), jnp.float32),
@@ -348,7 +399,9 @@
             pltpu.VMEM((n_z, strip, NB_SIGMA), jnp.float32),
             pltpu.VMEM((n_rel - 1, n_z * strip, NB_SIGMA), jnp.float32),
             pltpu.VMEM((n_z - 1, strip, NB_SIGMA), jnp.float32),
-            dma,
+            dma((2,)),
+            dma((2,)),
+            dma((2,)),
             dma((n_rel,)),
             dma((n_rel,)),
             dma((n_rel, n_z - 1)),
@@ -366,12 +419,10 @@
             collective_id=0, has_side_effects=True, vmem_limit_bytes=60 * 2**20
         ),
     )(
-        pair_density.reshape(slots * block, plane_rows),
+        pair_density.reshape(capacity * block, plane_rows),
         eigvecs,
         screening,
-        keep_rows.reshape(n_z, rows, 1),
-        jnp.broadcast_to(weights[:, None, None], (slots, 8, block))[:, :1],
-        window_start,
+        meta,
     )
 
 

time: 184 us -> 186 us (1.011)
  Pallas kernels: 178 us -> 182 us
    pallas_call x1, Pallas kernels: 178 us -> 182 us  [per_device(): pl.pallas_call(fused_kernel, out_shape=jax.ShapeDtypeStruct((strip, NB_SI...]
where the time goes in v3:
time: 186 us; the launch traced here: 185 us
  Pallas kernels  182 us (98%)
  local copies, waits for them, and re-layouts  2.16 us (1%)
    pallas_call x1, Pallas kernels, per_device(): pl.pallas_call(fused_kernel, out_shape=jax.ShapeDtypeStruct((strip, NB_SI...  182 us

profile of v3, /device:TPU:0, one launch (start us, length us, event | category | flops | bytes accessed | tf_op | source)
XLA Modules:
  0.0 185.3 jit_solution(10421937867896107679)
XLA Ops:
  0.0 0.9 select_reduce_fusion
  0.9 0.7 fusion.1
  1.6 0.1 copy.10
  1.7 0.7 broadcast_in_dim.25.meta_ref
  2.4 181.6 %shard_map.73 = f32[16,512]{1,0:T(8,128)} custom-call(bf16[640,2304]{1,0:T(8,128)(2,1)} %bitcast.7, bf16[368,2304]{1,0:T(8,128)(2,1)} %eig_ref.1, bf16[736,2944]{1,0:T(8,128)(2,1)} %screen_ref.1, f32[5,8,128]{2,1,0:T(8,128)} %broadcast_in_dim.25.meta_ref), custom_call_target="tpu_custom_call" | custom-call | tf_op jit(solution)/shard_map/pallas_call | solution.py:375
  184.0 1.4 copy.12
  (3 shorter events, 0.0 us)

commit v4 on v3

--- a/solution.py
+++ b/solution.py
@@ -72,7 +72,7 @@
     density_ref, eig_ref, screen_ref, meta_ref, out_ref,
     density, extra, extra_meta, meta, eig, screen, part, sent, own, landed, proj, acc,
     place, high, low, sigma, band_sum, sigma_in, band_in,
-    load_sem, extra_send, extra_recv, eig_send, eig_recv, red_send, red_recv, up_send, up_recv, down_send, down_recv,
+    load_sem, extra_send, extra_recv, half_send, half_recv, eig_send, eig_recv, red_send, red_recv, up_send, up_recv, down_send, down_recv,
     sig_send, sig_recv, fin_send, fin_recv,
 ):
     mesh_id = pl.DeviceIdType.MESH
@@ -98,6 +98,24 @@
         load.start()
     pl.semaphore_wait(barrier, n_rel - 1 + n_z - 1)
 
+    middle = -(-depth // 32) * 16
+    halves = (pl.ds(0, middle), pl.ds(middle, depth - middle))
+
+    def half_copy(rel, half):
+        return pltpu.make_async_remote_copy(
+            src_ref=eig_ref.at[halves[half]], dst_ref=eig.at[rel, halves[half]],
+            send_sem=half_send.at[half, rel], recv_sem=half_recv.at[half, rel],
+            device_id=(flip(band, rel), z), device_id_type=mesh_id,
+        )
+
+    def corner_copy(half):
+        via = (2, 4)[half]
+        return pltpu.make_async_remote_copy(
+            src_ref=eig.at[via, halves[half]], dst_ref=eig.at[6, halves[half]],
+            send_sem=half_send.at[half, 6], recv_sem=half_recv.at[half, 6],
+            device_id=(flip(band, 6 - via), z), device_id_type=mesh_id,
+        )
+
     def eig_copy(rel):
         return pltpu.make_async_remote_copy(
             src_ref=eig_ref, dst_ref=eig.at[rel], send_sem=eig_send.at[rel],
@@ -122,8 +140,9 @@
     ]
     for swap in swaps:
         swap.start()
-    for rel in (1, 2, 4, 6):
-        eig_copy(rel).start()
+    for rel, half in ((2, 0), (4, 1), (2, 1), (4, 0)):
+        half_copy(rel, half).start()
+    eig_copy(1).start()
     def red_copy(rel, k):
         target = lax.rem(z + k, n_z)
         return pltpu.make_async_remote_copy(
@@ -195,9 +214,26 @@
                 red_copy(rel, k).start()
 
     def project(rel):
-        @pl.when(rel >= 1)
+        @pl.when(lax.rem(rel, 2) == 1)
         def _():
             eig_copy(rel).wait_recv()
+
+        @pl.when(rel == 2)
+        def _():
+            half_copy(2, 0).wait_recv()
+            corner_copy(0).start()
+            half_copy(4, 1).wait_recv()
+            corner_copy(1).start()
+            half_copy(2, 1).wait_recv()
+
+        @pl.when(rel == 4)
+        def _():
+            half_copy(4, 0).wait_recv()
+
+        @pl.when(rel == 6)
+        def _():
+            corner_copy(0).wait_recv()
+            corner_copy(1).wait_recv()
 
         @pl.when((rel >= 2) & (lax.rem(rel, 2) == 0))
         def _():
@@ -335,8 +371,11 @@
 
     for swap in swaps:
         swap.wait_send()
-    for rel in (1, 2, 4, 6):
-        eig_copy(rel).wait_send()
+    eig_copy(1).wait_send()
+    for half in range(2):
+        corner_copy(half).wait_send()
+        for rel in (2, 4):
+            half_copy(rel, half).wait_send()
     for rel in (2, 4, 6):
         forward_copy(rel).wait_send()
 
@@ -402,6 +441,8 @@
             dma((2,)),
             dma((2,)),
             dma((2,)),
+            dma((2, n_rel)),
+            dma((2, n_rel)),
             dma((n_rel,)),
             dma((n_rel,)),
             dma((n_rel, n_z - 1)),

time: 186 us -> 159 us (0.85)
  Pallas kernels: 182 us -> 155 us
    pallas_call x1, Pallas kernels: 182 us -> 155 us  [per_device(): pl.pallas_call(fused_kernel, out_shape=jax.ShapeDtypeStruct((strip, NB_SI...]
where the time goes in v4:
time: 159 us
  Pallas kernels  155 us (97%)
  local copies, waits for them, and re-layouts  2.16 us (1%)
    pallas_call x1, Pallas kernels, per_device(): pl.pallas_call(fused_kernel, out_shape=jax.ShapeDtypeStruct((strip, NB_SI...  155 us

profile of v4, /device:TPU:0, one launch (start us, length us, event | category | flops | bytes accessed | tf_op | source)
XLA Modules:
  0.0 158.5 jit_solution(1294756576149673188)
XLA Ops:
  0.0 0.9 select_reduce_fusion
  0.9 0.7 fusion.1
  1.6 0.1 copy.10
  1.7 0.7 broadcast_in_dim.25.meta_ref
  2.4 154.8 %shard_map.73 = f32[16,512]{1,0:T(8,128)} custom-call(bf16[640,2304]{1,0:T(8,128)(2,1)} %bitcast.7, bf16[368,2304]{1,0:T(8,128)(2,1)} %eig_ref.1, bf16[736,2944]{1,0:T(8,128)(2,1)} %screen_ref.1, f32[5,8,128]{2,1,0:T(8,128)} %broadcast_in_dim.25.meta_ref), custom_call_target="tpu_custom_call" | custom-call | tf_op jit(solution)/shard_map/pallas_call | solution.py:414
  157.2 1.4 copy.12
  (3 shorter events, 0.0 us)
